TPU v7x, 32 devices: a whole 2x2x4 slice. The times are simulated.
32 devices in a mesh: copy: 4 (over y, x), fsdp: 2 (over core), cols: 4 (over z).
Axes of the slice: x: 2, y: 2, z: 4, core: 2. Of those that a mesh axis runs over, the one named last changes fastest.
Arguments:
- train_gate: float32 [8192, 8192], P(('copy', 'fsdp'), 'cols'), parts along dimension 0, may hold values from -0.1875 to 0.1875
- drift_gate: float32 [8192, 8192], P(('copy', 'fsdp'), 'cols'), parts along dimension 0, may hold values from -6 to 6
- spread_gate: float32 [8192, 8192], P(('copy', 'fsdp'), 'cols'), parts along dimension 0, may hold values from 0.1 to 10
- train_up: float32 [8192, 8192], P(('copy', 'fsdp'), 'cols'), parts along dimension 0, may hold values from -0.1875 to 0.1875
- drift_up: float32 [8192, 8192], P(('copy', 'fsdp'), 'cols'), parts along dimension 0, may hold values from -6 to 6
- spread_up: float32 [8192, 8192], P(('copy', 'fsdp'), 'cols'), parts along dimension 0, may hold values from 0.1 to 10
- norm_train: float32 [8192], P(('copy', 'fsdp', 'cols')), parts along dimension 0, may hold values from 0.25 to 1.75
- norm_step: float32 [8192], P(('copy', 'fsdp', 'cols')), parts along dimension 0, may hold values from -0.3 to 0.3
Outputs:
- serve_gate: bfloat16 [8192, 8192], P('copy', 'cols'), parts along dimension 0
- serve_up: bfloat16 [8192, 8192], P('copy', 'cols'), parts along dimension 0
- scale_gate: float32 [32768], P(('copy', 'cols')), parts along dimension 0
- scale_up: float32 [32768], P(('copy', 'cols')), parts along dimension 0
- serve_norm: bfloat16 [8192], P('copy'), parts along dimension 0
- fresh_gate: float32 [8192, 8192], P(('copy', 'fsdp'), 'cols'), parts along dimension 0
- fresh_up: float32 [8192, 8192], P(('copy', 'fsdp'), 'cols'), parts along dimension 0
There are 4 independent parts, one for each index of `copy`. A program takes and returns all parts, laid end to end along the dimension named above; each array names one. Nothing has to cross between parts.
All inputs are finite; a program needn't handle non-finite values.
Results may differ from a plain program's by a relative error of at most 0.001.
Values may be sent and summed in bfloat16 or wider, within the bound.
A program may use at most 192 MiB of HBM per device.

v0:
```python
import jax
import jax.numpy as jnp
from jax import lax
from jax.sharding import PartitionSpec as P

learn_rate = 0.02
decay_rate = 0.1
tiny_value = 1e-08


def body(train_gate, drift_gate, spread_gate, train_up, drift_up, spread_up, norm_train, norm_step):
    fresh_gate = train_gate - learn_rate * (
        drift_gate / (jnp.sqrt(spread_gate) + tiny_value) + decay_rate * train_gate
    )
    fresh_up = train_up - learn_rate * (
        drift_up / (jnp.sqrt(spread_up) + tiny_value) + decay_rate * train_up
    )
    total_gate, total_up = lax.psum(
        (jnp.sum(fresh_gate * fresh_gate, axis=0), jnp.sum(fresh_up * fresh_up, axis=0)), "fsdp"
    )
    scale_gate = jnp.sqrt(total_gate)
    scale_up = jnp.sqrt(total_up)
    narrow_gate, narrow_up = (
        (fresh_gate / scale_gate).astype(jnp.bfloat16),
        (fresh_up / scale_up).astype(jnp.bfloat16),
    )
    serve_gate, serve_up = (
        lax.all_gather(narrow_gate, "fsdp", axis=0, tiled=True),
        lax.all_gather(narrow_up, "fsdp", axis=0, tiled=True),
    )
    serve_norm = lax.all_gather(
        (norm_train + norm_step).astype(jnp.bfloat16), ("fsdp", "cols"), axis=0, tiled=True
    )
    return (serve_gate, serve_up, scale_gate, scale_up, serve_norm, fresh_gate, fresh_up)


def solution(mesh):
    return jax.shard_map(
        body,
        mesh=mesh,
        in_specs=(
            P(("copy", "fsdp"), "cols"),
            P(("copy", "fsdp"), "cols"),
            P(("copy", "fsdp"), "cols"),
            P(("copy", "fsdp"), "cols"),
            P(("copy", "fsdp"), "cols"),
            P(("copy", "fsdp"), "cols"),
            P(("copy", "fsdp", "cols")),
            P(("copy", "fsdp", "cols")),
        ),
        out_specs=(
            P("copy", "cols"),
            P("copy", "cols"),
            P(("copy", "cols")),
            P(("copy", "cols")),
            P("copy"),
            P(("copy", "fsdp"), "cols"),
            P(("copy", "fsdp"), "cols"),
        ),
        check_vma=False,
    )
```

profile of v0, /device:TPU:0, one launch (start us, length us, event | category | flops | bytes accessed | tf_op | source)
XLA Modules:
  0.0 111.6 jit_solution(9658315372463230520)
XLA Ops:
  7.2 0.0 all-gather.6.cloned.1.call-start
  7.2 24.8 %multiply_reduce_fusion = (f32[2048]{0:T(1024)S(1)}, f32[1024,2048]{1,0:T(8,128)}, f32[2048]{0:T(1024)S(1)}, f32[1024,2048]{1,0:T(8,128)}) fusion(f32[1024,2048]{1,0:T(8,128)} %param.11, f32[1024,2048]{1,0:T(8,128)} %param.12, f32[1024,2048]{1,0:T(8,128)} %param.13, f32[1024,2048]{1,0:T(8,128)} %param.8, f32[1024,2048]{1,0:T(8,128)} %param.9, ...), kind=kLoop, calls=%fused_computation.1 | loop fusion | flops 33550336 | bytes 67125248 | tf_op jit(solution)/shard_map/reduce_sum | solution.py:19
  32.0 3.6 %all-reduce = (f32[2048]{0:T(1024)S(1)}, f32[2048]{0:T(1024)S(1)}) all-reduce(f32[2048]{0:T(1024)S(1)} %get-tuple-element.13, f32[2048]{0:T(1024)S(1)} %get-tuple-element.9), channel_id=1, replica_groups=mesh['copy'=4,'fsdp'=2,'cols'=4] {'fsdp'}, use_global_device_ids=true, to_apply=%region_1.0 | all-reduce | flops 4096 | bytes 32768 | tf_op jit(solution)/shard_map/psum | solution.py:18
  35.7 0.0 copy-start
  35.7 6.6 %divide_convert_fusion = bf16[1024,2048]{1,0:T(8,128)(2,1)} fusion(f32[1024,2048]{1,0:T(8,128)} %get-tuple-element.28, f32[2048]{0:T(1024)S(1)} %sqrt.15), kind=kLoop, calls=%fused_computation | loop fusion | flops 4194304 | bytes 12591104 | tf_op jit(solution)/shard_map/convert_element_type | solution.py:25
  42.2 0.0 all-gather.6.cloned.1.call-update
  42.3 0.0 copy-done
  42.3 0.0 all-gather.4.cloned.1.call-start
  42.3 0.0 copy-start.1
  42.4 0.0 copy-start.2
  42.4 0.0 copy-start.3
  42.4 6.6 %divide_convert_fusion.1 = bf16[1024,2048]{1,0:T(8,128)(2,1)} fusion(f32[1024,2048]{1,0:T(8,128)} %get-tuple-element.27, f32[2048]{0:T(1024)S(1)} %sqrt.13), kind=kLoop, calls=%fused_computation.3 | loop fusion | flops 4194304 | bytes 12591104 | tf_op jit(solution)/shard_map/convert_element_type | solution.py:24
  49.0 0.0 all-gather.4.cloned.1.call-update
  49.0 0.0 copy-done.1
  49.0 0.0 copy-done.2
  49.0 0.0 copy-done.3
  49.0 17.5 %all-gather = bf16[8,1,256]{2,1,0:T(2,128)(2,1)S(1)} all-gather(bf16[1,1,256]{2,1,0:T(2,128)(2,1)S(1)} %reshape.16), channel_id=1, replica_groups=mesh['copy'=4,'fsdp'=2,'cols'=4] {'fsdp','cols'}, dimensions={0}, use_global_device_ids=true | all-gather | bytes 4608 | tf_op jit(solution)/shard_map/all_gather | solution.py:31
  66.5 0.6 copy.15
  67.1 0.0 all-gather.6.cloned.1.call-done
  67.1 20.7 %all-gather.4.cloned.1.call-done = bf16[2048,2048]{1,0:T(8,128)(2,1)} async-done(((bf16[1024,2048]{1,0:T(8,128)(2,1)}), bf16[2048,2048]{1,0:T(8,128)(2,1)}) %all-gather.4.cloned.1.call-update) | async-done | bytes 8388624 | tf_op jit(solution)/shard_map/all_gather | solution.py:28
  87.9 8.4 %copy.18 = bf16[2048,2048]{1,0:T(8,128)(2,1)} copy(bf16[2048,2048]{1,0:T(8,128)(2,1)} %all-gather.4.cloned.1.call-done) | data formatting | bytes 16777216
  96.3 8.4 %copy.19 = bf16[2048,2048]{1,0:T(8,128)(2,1)} copy(bf16[2048,2048]{1,0:T(8,128)(2,1)} %all-gather.6.cloned.1.call-done) | data formatting | bytes 16777216
  (5 shorter events, 0.1 us)
Async XLA Ops:
  7.2 60.0 %all-gather.6.cloned.1.call-start = ((), (), s32[]{:S(2)}) async-start(), calls=%async_computation.1 | async-start | bytes 12582912 | tf_op jit(solution)/shard_map/all_gather | solution.py:29
  35.7 6.6 %copy-start = (f32[2048]{0:T(1024)}, f32[2048]{0:T(1024)S(1)}, u32[]{:S(2)}) copy-start(f32[2048]{0:T(1024)S(1)} %sqrt.15) | copy-start | bytes 24580
  42.3 45.6 %all-gather.4.cloned.1.call-start = ((), (), s32[]{:S(2)}) async-start(), calls=%async_computation | async-start | bytes 12582912 | tf_op jit(solution)/shard_map/all_gather | solution.py:28
  42.3 6.6 %copy-start.1 = (f32[2048]{0:T(1024)}, f32[2048]{0:T(1024)S(1)}, u32[]{:S(2)}) copy-start(f32[2048]{0:T(1024)S(1)} %sqrt.13) | copy-start | bytes 24580
  42.4 6.6 %copy-start.2 = (f32[256]{0:T(256)S(1)}, f32[256]{0:T(256)}, u32[]{:S(2)}) copy-start(f32[256]{0:T(256)} %param.14) | copy-start | bytes 3076
  42.4 6.6 %copy-start.3 = (f32[256]{0:T(256)S(1)}, f32[256]{0:T(256)}, u32[]{:S(2)}) copy-start(f32[256]{0:T(256)} %param.15) | copy-start | bytes 3076
Sparse Core Ops, SparseCore 0:
  42.4 22.2 all-gather.5
  66.8 21.0 all-gather.3
where the time goes:
time: 112 us
  other arithmetic  38 us (34%)
  blocking collectives  21.1 us (19%)
  waiting for transfers between devices  20.7 us (18%)
  local copies, waits for them, and re-layouts  17.5 us (16%)
  between operations  14.1 us (13%)
    reduce_sum x1, other arithmetic, body(): jnp.sum(fresh_up * fresh_up, axis=0)  24.8 us
    all_gather x1, waiting for transfers between devices, body(): lax.all_gather(narrow_gate, 'fsdp', axis=0, tiled=True)  20.7 us
    unnamed x12, local copies, waits for them, and re-layouts  17.5 us
    all_gather x1, blocking collectives, body(): lax.all_gather((norm_train + norm_step).astype(jnp.bfloat16), ('fsdp', 'c...  17.5 us
    convert_element_type x1, other arithmetic, body(): (fresh_gate / scale_gate).astype(jnp.bfloat16)  6.58 us
    convert_element_type x1, other arithmetic, body(): (fresh_up / scale_up).astype(jnp.bfloat16)  6.58 us
    psum x1, blocking collectives, body(): lax.psum((jnp.sum(fresh_gate * fresh_gate, axis=0), jnp.sum(fresh_up * fr...  3.6 us
  transfers between devices with their start and end apart: 2, of which 1 were waited for; matrix products, arithmetic and copies ran while one was open for 6% of the time, Pallas kernels for 0%

commit v1 on v0

v1 whole, which is shorter than its diff:
```python
import functools

import jax
import jax.numpy as jnp
from jax import lax
from jax.experimental import pallas as pl
from jax.experimental.pallas import tpu as pltpu
from jax.sharding import PartitionSpec as P

learn_rate = 0.02
decay_rate = 0.1
tiny_value = 1e-08

LANES = 128
SUBLANES = 8
SLOTS = 3
WIDTH = 256
ROWS = 32
MESH = pl.DeviceIdType.MESH


def step_kernel(sizes, *refs):
    share, across, rows, columns, width = sizes
    group = share * across
    chunks = columns // width
    steps = 2 * chunks
    sources = (refs[0:3], refs[3:6])
    norm_ref = refs[6]
    fresh_ref, serve_ref, scale_ref, norm_out = refs[7:11]
    inbox, sums, in_sem, sum_send, sum_recv, half_send, half_recv, norm_send, norm_recv = refs[11:]
    me = lax.axis_index("fsdp")
    column = lax.axis_index("cols")
    place = me * across + column

    def start_input(which, slot, index):
        offset = pl.multiple_of(index * width, width)
        for k in range(3):
            pltpu.make_async_copy(
                sources[which][k].at[:, pl.ds(offset, width)], inbox.at[slot, k], in_sem.at[slot, k]
            ).start()

    def begin(c):
        slot = lax.rem(c, SLOTS)

        @pl.when(c < chunks)
        def _():
            start_input(0, slot, c)

        @pl.when(c >= chunks)
        def _():
            start_input(1, slot, c - chunks)

    def sum_copy(c, k):
        return pltpu.make_async_remote_copy(
            src_ref=sums.at[c, me],
            dst_ref=sums.at[c, me],
            send_sem=sum_send.at[c, k - 1],
            recv_sem=sum_recv.at[c, k - 1],
            device_id={"fsdp": lax.rem(me + k, share)},
            device_id_type=MESH,
        )

    def half_copy(c, k):
        part = serve_ref.at[
            c // chunks,
            pl.ds(pl.multiple_of(me * rows, rows), rows),
            pl.ds(pl.multiple_of(lax.rem(c, chunks) * width, width), width),
        ]
        return pltpu.make_async_remote_copy(
            src_ref=part,
            dst_ref=part,
            send_sem=half_send.at[c, k - 1],
            recv_sem=half_recv.at[c, k - 1],
            device_id={"fsdp": lax.rem(me + k, share)},
            device_id_type=MESH,
        )

    def norm_copy(k):
        other = lax.rem(place + k, group)
        return pltpu.make_async_remote_copy(
            src_ref=norm_out.at[place],
            dst_ref=norm_out.at[place],
            send_sem=norm_send.at[k - 1],
            recv_sem=norm_recv.at[k - 1],
            device_id={"fsdp": other // across, "cols": lax.rem(other, across)},
            device_id_type=MESH,
        )

    for c in range(min(SLOTS, steps)):
        start_input(c // chunks, c, c % chunks)

    barrier = pltpu.get_barrier_semaphore()
    for k in range(1, group):
        other = lax.rem(place + k, group)
        pl.semaphore_signal(
            barrier,
            inc=1,
            device_id={"fsdp": other // across, "cols": lax.rem(other, across)},
            device_id_type=MESH,
        )
    norm_out[place] = norm_ref[...]
    pl.semaphore_wait(barrier, group - 1)
    for k in range(1, group):
        norm_copy(k).start()

    def compute(c):
        slot = lax.rem(c, SLOTS)
        which = c // chunks
        offset = pl.multiple_of(lax.rem(c, chunks) * width, width)
        for k in range(3):
            pltpu.make_async_copy(
                sources[0][k].at[:, pl.ds(0, width)], inbox.at[slot, k], in_sem.at[slot, k]
            ).wait()

        def block(i, total):
            at = pl.ds(pl.multiple_of(i * ROWS, ROWS), ROWS)
            train = inbox[slot, 0, at, :]
            drift = inbox[slot, 1, at, :]
            spread = inbox[slot, 2, at, :]
            root = spread * lax.rsqrt(spread)
            fresh = train * (1.0 - learn_rate * decay_rate) - learn_rate * (
                drift / (root + tiny_value)
            )
            fresh_ref[which, at, pl.ds(offset, width)] = fresh
            square = (fresh * fresh).reshape(ROWS // SUBLANES, SUBLANES, width)
            return total + jnp.sum(square, axis=0)

        sums[c, me] = lax.fori_loop(
            0, rows // ROWS, block, jnp.zeros((SUBLANES, width), jnp.float32), unroll=2
        )
        for k in range(1, share):
            sum_copy(c, k).start()

        @pl.when(c + SLOTS < steps)
        def _():
            begin(c + SLOTS)

    def narrow(c):
        which = c // chunks
        offset = pl.multiple_of(lax.rem(c, chunks) * width, width)
        for k in range(1, share):
            sum_copy(c, k).wait_recv()
        total = sums[c, 0]
        for j in range(1, share):
            total += sums[c, j]
        scale = jnp.sqrt(jnp.sum(total, axis=0, keepdims=True))
        for j in range(width // LANES):
            scale_ref[pl.ds(c * (width // LANES) + j, 1), :] = scale[:, j * LANES : (j + 1) * LANES]
        inverse = 1.0 / scale

        def block(i, carry):
            at = pl.ds(pl.multiple_of(i * ROWS, ROWS), ROWS)
            to = pl.ds(pl.multiple_of(me * rows + i * ROWS, ROWS), ROWS)
            serve_ref[which, to, pl.ds(offset, width)] = (
                fresh_ref[which, at, pl.ds(offset, width)] * inverse
            ).astype(jnp.bfloat16)
            return carry

        lax.fori_loop(0, rows // ROWS, block, 0, unroll=2)
        for k in range(1, share):
            half_copy(c, k).start()

    def step(c, carry):
        @pl.when(c < steps)
        def _():
            compute(c)

        @pl.when(c >= 1)
        def _():
            narrow(c - 1)

        return carry

    lax.fori_loop(0, steps + 1, step, 0)

    for k in range(1, group):
        norm_copy(k).wait()

    def finish(c, carry):
        for k in range(1, share):
            sum_copy(c, k).wait_send()
            half_copy(c, k).wait()
        return carry

    lax.fori_loop(0, steps, finish, 0)


def write_kernel(fresh_ref, serve_ref, scale_ref, *refs):
    outs, sem = refs[:6], refs[6]
    half = scale_ref.shape[0] // 2
    copies = [
        pltpu.make_async_copy(source, target, sem.at[n])
        for n, (source, target) in enumerate(
            zip(
                (
                    fresh_ref.at[0],
                    fresh_ref.at[1],
                    serve_ref.at[0],
                    serve_ref.at[1],
                    scale_ref.at[pl.ds(0, half)],
                    scale_ref.at[pl.ds(half, half)],
                ),
                outs,
            )
        )
    ]
    for copy in copies:
        copy.start()
    for copy in copies:
        copy.wait()


def body(share, across, train_gate, drift_gate, spread_gate, train_up, drift_up, spread_up, norm_train, norm_step):
    rows, columns = train_gate.shape
    group = share * across
    steps = 2 * columns // WIDTH
    piece = norm_train.shape[0]
    tile = SUBLANES * LANES
    padded = -(-piece // tile) * tile
    norm = jnp.pad(norm_train + norm_step, (0, padded - piece)).reshape(padded // LANES, LANES)
    big = (train_gate, drift_gate, spread_gate, train_up, drift_up, spread_up)
    vmem = pl.BlockSpec(memory_space=pltpu.VMEM)
    hbm = pl.BlockSpec(memory_space=pltpu.HBM)
    fresh, serve, scale, norms = pl.pallas_call(
        functools.partial(step_kernel, (share, across, rows, columns, WIDTH)),
        out_shape=(
            pltpu.VMEM((2, rows, columns), jnp.float32),
            pltpu.VMEM((2, share * rows, columns), jnp.bfloat16),
            pltpu.VMEM((2 * columns // LANES, LANES), jnp.float32),
            pltpu.VMEM((group, padded // LANES, LANES), jnp.float32),
        ),
        in_specs=[hbm] * 6 + [vmem],
        out_specs=(vmem,) * 4,
        scratch_shapes=[
            pltpu.VMEM((SLOTS, 3, rows, WIDTH), jnp.float32),
            pltpu.VMEM((steps, share, SUBLANES, WIDTH), jnp.float32),
            pltpu.SemaphoreType.DMA((SLOTS, 3)),
            pltpu.SemaphoreType.DMA((steps, share - 1)),
            pltpu.SemaphoreType.DMA((steps, share - 1)),
            pltpu.SemaphoreType.DMA((steps, share - 1)),
            pltpu.SemaphoreType.DMA((steps, share - 1)),
            pltpu.SemaphoreType.DMA((group - 1,)),
            pltpu.SemaphoreType.DMA((group - 1,)),
        ],
        compiler_params=pltpu.CompilerParams(
            collective_id=0, has_side_effects=True, vmem_limit_bytes=12 * 2**20
        ),
        name="step_kernel",
    )(*[pltpu.with_memory_space_constraint(x, pltpu.HBM) for x in big], norm)
    held = [pltpu.with_memory_space_constraint(x, pltpu.VMEM) for x in (fresh, serve, scale)]
    fresh_gate, fresh_up, serve_gate, serve_up, scale_gate, scale_up = pl.pallas_call(
        write_kernel,
        out_shape=(
            pltpu.HBM((rows, columns), jnp.float32),
            pltpu.HBM((rows, columns), jnp.float32),
            pltpu.HBM((share * rows, columns), jnp.bfloat16),
            pltpu.HBM((share * rows, columns), jnp.bfloat16),
            pltpu.HBM((columns // LANES, LANES), jnp.float32),
            pltpu.HBM((columns // LANES, LANES), jnp.float32),
        ),
        in_specs=[vmem] * 3,
        out_specs=(hbm,) * 6,
        scratch_shapes=[pltpu.SemaphoreType.DMA((6,))],
        compiler_params=pltpu.CompilerParams(vmem_limit_bytes=2**20),
        name="write_kernel",
    )(*held)
    serve_norm = norms.reshape(group, padded)[:, :piece].reshape(group * piece).astype(jnp.bfloat16)
    return (
        serve_gate,
        serve_up,
        scale_gate.reshape(columns),
        scale_up.reshape(columns),
        serve_norm,
        fresh_gate,
        fresh_up,
    )


def solution(mesh):
    share, across = mesh.shape["fsdp"], mesh.shape["cols"]
    weight = P(("copy", "fsdp"), "cols")
    gain = P(("copy", "fsdp", "cols"))
    return jax.shard_map(
        functools.partial(body, share, across),
        mesh=mesh,
        in_specs=(weight,) * 6 + (gain, gain),
        out_specs=(
            P("copy", "cols"),
            P("copy", "cols"),
            P(("copy", "cols")),
            P(("copy", "cols")),
            P("copy"),
            weight,
            weight,
        ),
        check_vma=False,
    )
```

time: 112 us -> 37.1 us (0.33)
  other arithmetic: 38 us -> 0.7 us
  Pallas kernels: 0 us -> 34.9 us
  blocking collectives: 21.1 us -> 0 us
  waiting for transfers between devices: 20.7 us -> 0 us
  local copies, waits for them, and re-layouts: 17.5 us -> 0.61 us
  between operations: 14.1 us -> 0.67 us
    pallas_call x0 -> x2, Pallas kernels: none -> 34.9 us  [the longest x1 23.6 us: body(): pl.pallas_call(functools.partial(step_kernel, (share, across, rows, colum...]
    reduce_sum x1 -> x0, other arithmetic: 24.8 us -> none  [body(): jnp.sum(fresh_up * fresh_up, axis=0)]
    all_gather x2 -> x0, waiting for transfers between devices: 20.7 us -> none  [the longest x1 20.7 us: body(): lax.all_gather(narrow_gate, 'fsdp', axis=0, tiled=True)]
    all_gather x1 -> x0, blocking collectives: 17.5 us -> none  [body(): lax.all_gather((norm_train + norm_step).astype(jnp.bfloat16), ('fsdp', 'c...]
    unnamed x12 -> x3, local copies, waits for them, and re-layouts: 17.5 us -> 0.6 us
    convert_element_type x3 -> x0, other arithmetic: 13.2 us -> none  [the longest x1 6.58 us: body(): (fresh_gate / scale_gate).astype(jnp.bfloat16)]
    psum x1 -> x0, blocking collectives: 3.6 us -> none  [body(): lax.psum((jnp.sum(fresh_gate * fresh_gate, axis=0), jnp.sum(fresh_up * fr...]
  transfers between devices with their start and end apart: 2 -> 0, of which waited for: 1 -> 0; matrix products, arithmetic and copies ran while one was open for 6% -> 0% of each run, Pallas kernels for 0% -> 0%
where the time goes in v1:
time: 37.1 us; the launch traced here: 36.9 us
  Pallas kernels  34.9 us (94%)
  other arithmetic  0.7 us (2%)
  between operations  0.67 us (2%)
  local copies, waits for them, and re-layouts  0.61 us (2%)
    pallas_call x1, Pallas kernels, body(): pl.pallas_call(functools.partial(step_kernel, (share, across, rows, colum...  23.6 us
    pallas_call x1, Pallas kernels, body(): pl.pallas_call(write_kernel, out_shape=(pltpu.HBM((rows, columns), jnp.fl...  11.3 us

profile of v1, /device:TPU:0, one launch (start us, length us, event | category | flops | bytes accessed | tf_op | source)
XLA Modules:
  0.0 36.9 jit_solution(11254504506802051878)
XLA Ops:
  0.6 0.7 %add.5 = f32[256]{0:T(256)S(1)} add(f32[256]{0:T(256)} %param.14, f32[256]{0:T(256)} %param.15) | non-fusion elementwise | flops 256 | bytes 3072 | tf_op jit(solution)/shard_map/add | solution.py:220
  1.3 23.6 %step_kernel.1 = (f32[2,1024,2048]{2,1,0:T(8,128)S(1)}, bf16[2,2048,2048]{2,1,0:T(8,128)(2,1)S(1)}, f32[32,128]{1,0:T(8,128)S(1)}, f32[8,8,128]{2,1,0:T(8,128)S(1)}) custom-call(f32[1024,2048]{1,0:T(8,128)} %refs_0_.1, f32[1024,2048]{1,0:T(8,128)} %refs_1_.1, f32[1024,2048]{1,0:T(8,128)} %refs_2_.1, f32[1024,2048]{1,0:T(8,128)} %refs_3_.1, ...), custom_call_target="tpu_custom_call" | custom-call | tf_op jit(solution)/shard_map/step_kernel/pallas_call | solution.py:224
  25.0 11.3 %write_kernel.1 = (f32[1024,2048]{1,0:T(8,128)}, f32[1024,2048]{1,0:T(8,128)}, bf16[2048,2048]{1,0:T(8,128)(2,1)}, bf16[2048,2048]{1,0:T(8,128)(2,1)}, f32[16,128]{1,0:T(8,128)}, /*index=5*/f32[16,128]{1,0:T(8,128)}) custom-call(f32[2,1024,2048]{2,1,0:T(8,128)S(1)} %get-tuple-element.17.fresh_ref, bf16[2,2048,2048]{2,1,0:T(8,128)(2,1)S(1)} %get-tuple-element.18.serve_ref, ...), custom_call_target="tpu_custom_call" | custom-call | tf_op jit(solution)/shard_map/write_kernel/pallas_call | solution.py:251
  36.3 0.6 %copy.16 = bf16[1,2,8,128]{3,1,2,0:T(2,128)(2,1)} copy(bf16[1,2,8,128]{3,2,1,0:T(8,128)(2,1)S(1)} %slice_bitcast_fusion) | data formatting | bytes 8192
  (4 shorter events, 0.0 us)
